TPU v7x, 8 devices: a whole 2x2x1 slice. The times are simulated.
8 devices in a mesh: rep: 1 (over z), dp: 8 (over x, y, core).
Axes of the slice: x: 2, y: 2, z: 1, core: 2. Of those that a mesh axis runs over, the one named last changes fastest.
Arguments:
- a: bfloat16 [8, 4, 4096, 1536], P(('rep', 'dp'))
- g: bfloat16 [8, 4, 4096, 4224], P(('rep', 'dp'))
Outputs:
- output: bfloat16 [4, 1536, 4224], P('rep')
All inputs are finite; a program needn't handle non-finite values.
Results may differ from a plain program's by a relative error of at most 0.012.
Values are sent between devices in bfloat16 or wider.
A program may use at most 2 GiB of HBM per device.

v0:
```python
import jax
import jax.numpy as jnp


def solution(mesh):
    groups = mesh.shape["rep"]

    def step(a, g):
        a, g = (t.reshape(groups, -1, *t.shape[1:]) for t in (a, g))
        sums = jnp.einsum("rsntd,rsntf->rndf", a, g, preferred_element_type=jnp.float32)
        return sums.astype(jnp.bfloat16).reshape(-1, *sums.shape[2:])

    return step
```

profile of v0, /device:TPU:0, one launch (start us, length us, event | category | flops | bytes accessed | tf_op | source)
XLA Modules:
  0.0 1448.0 jit_solution(16143101214220339510)
XLA Ops:
  0.0 248.9 %fusion = f32[4,1536,4224]{2,1,0:T(8,128)} fusion(bf16[1,4,4096,4224]{3,2,1,0:T(8,128)(2,1)} %param.1, bf16[1,4,4096,1536]{3,2,1,0:T(8,128)(2,1)} %param), kind=kOutput, calls=%fused_computation | convolution fusion | flops 212600881152 | bytes 292552704 | tf_op jit(solution)/rsntd,rsntf->rndf/dot_general | solution.py:10
  248.9 1199.1 %all-reduce.2 = bf16[4,1536,4224]{2,1,0:T(8,128)(2,1)} all-reduce(f32[4,1536,4224]{2,1,0:T(8,128)} %fusion), channel_id=1, replica_groups=mesh['axis_0'=8] {'axis_0'}, use_global_device_ids=true, to_apply=%add.clone | all-reduce | flops 25952256 | bytes 155713536 | tf_op jit(solution)/rsntd,rsntf->rndf/dot_general | solution.py:10
where the time goes:
time: 1450 us
  blocking collectives  1200 us (83%)
  matrix products  249 us (17%)
    dot_general x1, blocking collectives, step(): jnp.einsum('rsntd,rsntf->rndf', a, g, preferred_element_type=jnp.float32)  1200 us
    dot_general x1, matrix products, step(): jnp.einsum('rsntd,rsntf->rndf', a, g, preferred_element_type=jnp.float32)  249 us

commit v1 on v0

v1 whole, which is shorter than its diff:
```python
import jax
import jax.numpy as jnp
from jax import lax
from jax.experimental import pallas as pl
from jax.experimental.pallas import tpu as pltpu
from jax.sharding import PartitionSpec as P

MESH = pl.DeviceIdType.MESH
W = 256
G_SLOTS = 3
F32, BF16 = jnp.float32, jnp.bfloat16
LAG2, LAG3, LAG4, LAG5, LAG6 = 1, 2, 3, 5, 7


def _kernel(
    a, g, out,
    a_buf, g_buf, pair_send, own, pair_recv,
    send1, keep1, recv1, send2, keep2, recv2, fin,
    a_sem, g_sem, pair_ss, pair_rs, ss1, rs1, ss2, rs2, loc, gs1, gr1, gs2, gr2, fs, fr,
):
    mats, rows, cols = out.shape
    half, quarter = rows // 2, rows // 8
    eighth = quarter // 2
    per = pl.cdiv(cols, W)
    last_w = cols - (per - 1) * W
    chunks = mats * per

    me = lax.axis_index("dp")
    c, y, x = lax.rem(me, 2), lax.rem(me // 2, 2), me // 4
    xn = {"dp": (1 - x) * 4 + y * 2 + c}
    yn = {"dp": x * 4 + (1 - y) * 2 + c}
    pn = {"dp": x * 4 + y * 2 + (1 - c)}

    barrier = pltpu.get_barrier_semaphore()
    for d in (xn, yn, pn):
        pl.semaphore_signal(barrier, inc=1, device_id=d, device_id_type=MESH)

    base = c * half
    p_mine, p_other = quarter * x, quarter * (1 - x)
    q_mine, q_other = 2 * quarter + quarter * y, 2 * quarter + quarter * (1 - y)

    def by_width(k, fn):
        if last_w == W:
            fn(W)
            return
        j = lax.rem(k, per)
        pl.when(j < per - 1)(lambda: fn(W))
        pl.when(j == per - 1)(lambda: fn(last_w))

    def where(k, w, start, size):
        start = pl.multiple_of(start, eighth)
        col = pl.multiple_of(lax.rem(k, per) * W, W)
        return out.at[k // per, pl.ds(start, size), pl.ds(col, w)]

    def remote(src, dst, ss, rs, to):
        return pltpu.make_async_remote_copy(
            src_ref=src, dst_ref=dst, send_sem=ss, recv_sem=rs, device_id=to, device_id_type=MESH
        )

    def load_a(n, h):
        lanes = pl.ds(pl.multiple_of(h * half, half), half)
        slot = lax.rem(n, 2)
        return pltpu.make_async_copy(a.at[0, n, :, lanes], a_buf.at[slot, :, lanes], a_sem.at[slot, h])

    def load_g(k, w):
        slot = lax.rem(k, G_SLOTS)
        col = pl.multiple_of(lax.rem(k, per) * W, W)
        return pltpu.make_async_copy(
            g.at[0, k // per, :, pl.ds(col, w)], g_buf.at[slot, :, pl.ds(0, w)], g_sem.at[slot]
        )

    def pair(k, w):
        s, r = lax.rem(k, 2), lax.rem(k, 4)
        return remote(
            pair_send.at[s, :, pl.ds(0, w)], pair_recv.at[r, :, pl.ds(0, w)], pair_ss.at[s], pair_rs.at[r], pn
        )

    def scatter1(k, w):
        s = lax.rem(k, 4)
        return [
            remote(send1.at[s, i, :, pl.ds(0, w)], recv1.at[s, i, :, pl.ds(0, w)], ss1.at[s, i], rs1.at[s, i], d)
            for i, d in enumerate((xn, yn))
        ]

    def scatter2(k, w):
        s = lax.rem(k, 4)
        return [
            remote(send2.at[s, i, :, pl.ds(0, w)], recv2.at[s, i, :, pl.ds(0, w)], ss2.at[s, i], rs2.at[s, i], d)
            for i, d in enumerate((yn, xn))
        ]

    def final_rows():
        return (base + p_mine + eighth * y, base + q_mine + eighth * x)

    def keep_local(k, w):
        s = lax.rem(k, 4)
        return [
            pltpu.make_async_copy(fin.at[s, i, :, pl.ds(0, w)], where(k, w, r, eighth), loc.at[s, i])
            for i, r in enumerate(final_rows())
        ]

    def gather1(k, w):
        s, t = lax.rem(k, 4), lax.rem(k, 8)
        return [
            remote(fin.at[s, i, :, pl.ds(0, w)], where(k, w, r, eighth), gs1.at[t, i], gr1.at[t, i], d)
            for i, (r, d) in enumerate(zip(final_rows(), (yn, xn)))
        ]

    def gather2(k, w):
        t = lax.rem(k, 8)
        return [
            remote(where(k, w, r, quarter), where(k, w, r, quarter), gs2.at[t, i], gr2.at[t, i], d)
            for i, (r, d) in enumerate(((base + p_mine, xn), (base + q_mine, yn)))
        ]

    def exchange(k, w):
        t = lax.rem(k, 8)
        return remote(where(k, w, base, half), where(k, w, base, half), fs.at[t], fr.at[t], pn)

    def matmul(k, h):
        lanes = pl.ds(pl.multiple_of(h * half, half), half)
        return lax.dot_general(
            a_buf[lax.rem(k // per, 2), :, lanes],
            g_buf[lax.rem(k, G_SLOTS)],
            (((0,), (0,)), ((), ())),
            preferred_element_type=F32,
        )

    def start(copies):
        for copy in copies:
            copy.start()

    load_a(0, 1 - c).start()
    load_g(0, W).start()
    load_a(0, c).start()
    for k in range(1, G_SLOTS - 1):
        load_g(k, W).start()
    pl.semaphore_wait(barrier, 3)

    def compute(k):
        n, j = k // per, lax.rem(k, per)

        @pl.when(k + G_SLOTS - 1 < chunks)
        def _():
            by_width(k + G_SLOTS - 1, lambda w: load_g(k + G_SLOTS - 1, w).start())

        @pl.when((j == 1) & (n + 1 < mats))
        def _():
            load_a(n + 1, 1 - c).start()
            load_a(n + 1, c).start()

        pl.when(j == 0)(lambda: load_a(n, 1 - c).wait())
        by_width(k, lambda w: load_g(k, w).wait())
        pair_send[lax.rem(k, 2)] = matmul(k, 1 - c).astype(BF16)
        by_width(k, lambda w: pair(k, w).start())
        pl.when(j == 0)(lambda: load_a(n, c).wait())
        own[...] = matmul(k, c)

        by_width(k, lambda w: pair(k, w).wait_recv())
        r, s, kept = lax.rem(k, 4), lax.rem(k, 4), lax.rem(k, 2)

        def total(first):
            span = pl.ds(pl.multiple_of(first, quarter), quarter)
            return own[span, :] + pair_recv[r, span, :].astype(F32)

        send1[s, 0] = total(p_other).astype(BF16)
        send1[s, 1] = total(q_other).astype(BF16)
        by_width(k, lambda w: start(scatter1(k, w)))
        keep1[kept, 0] = total(p_mine)
        keep1[kept, 1] = total(q_mine)

    def second(k):
        def wait(w):
            pair(k, w).wait_send()
            for copy in scatter1(k, w):
                copy.wait_recv()

        by_width(k, wait)
        s, kept = lax.rem(k, 4), lax.rem(k, 2)
        for i, bit in enumerate((y, x)):
            def total(first):
                span = pl.ds(pl.multiple_of(first, eighth), eighth)
                return keep1[kept, i, span, :] + recv1[s, i, span, :].astype(F32)

            send2[s, i] = total(eighth * (1 - bit)).astype(BF16)
            keep2[kept, i] = total(eighth * bit)
        by_width(k, lambda w: start(scatter2(k, w)))

    def third(k):
        def wait(w):
            for copy in scatter1(k, w):
                copy.wait_send()
            for copy in scatter2(k, w):
                copy.wait_recv()

        by_width(k, wait)
        s, kept = lax.rem(k, 4), lax.rem(k, 2)
        for i in range(2):
            fin[s, i] = (keep2[kept, i] + recv2[s, i].astype(F32)).astype(BF16)
        by_width(k, lambda w: start(gather1(k, w) + keep_local(k, w)))

    def fourth(k):
        def go(w):
            for copy in scatter2(k, w):
                copy.wait_send()
            for copy in keep_local(k, w):
                copy.wait()
            for copy in gather1(k, w):
                copy.wait_recv()
            start(gather2(k, w))

        by_width(k, go)

    def fifth(k):
        def go(w):
            for copy in gather1(k, w):
                copy.wait_send()
            for copy in gather2(k, w):
                copy.wait_recv()
            exchange(k, w).start()

        by_width(k, go)

    def sixth(k):
        def go(w):
            for copy in gather2(k, w):
                copy.wait_send()
            exchange(k, w).wait()

        by_width(k, go)

    @pl.loop(0, chunks + LAG6)
    def _(i):
        pl.when(i < chunks)(lambda: compute(i))
        for lag, stage in ((LAG2, second), (LAG3, third), (LAG4, fourth), (LAG5, fifth), (LAG6, sixth)):
            pl.when((i >= lag) & (i < chunks + lag))(lambda lag=lag, stage=stage: stage(i - lag))


def solution(mesh):
    def body(a, g):
        mats, tokens, rows = a.shape[1:]
        cols = g.shape[-1]
        half, quarter = rows // 2, rows // 8
        eighth = quarter // 2
        dma = pltpu.SemaphoreType.DMA
        any_space = pl.BlockSpec(memory_space=pl.ANY)
        return pl.pallas_call(
            _kernel,
            out_shape=jax.ShapeDtypeStruct((mats, rows, cols), BF16),
            in_specs=[any_space, any_space],
            out_specs=any_space,
            scratch_shapes=[
                pltpu.VMEM((2, tokens, rows), BF16),
                pltpu.VMEM((G_SLOTS, tokens, W), BF16),
                pltpu.VMEM((2, half, W), BF16),
                pltpu.VMEM((half, W), F32),
                pltpu.VMEM((4, half, W), BF16),
                pltpu.VMEM((4, 2, quarter, W), BF16),
                pltpu.VMEM((2, 2, quarter, W), F32),
                pltpu.VMEM((4, 2, quarter, W), BF16),
                pltpu.VMEM((4, 2, eighth, W), BF16),
                pltpu.VMEM((2, 2, eighth, W), F32),
                pltpu.VMEM((4, 2, eighth, W), BF16),
                pltpu.VMEM((4, 2, eighth, W), BF16),
                dma((2, 2)), dma((G_SLOTS,)), dma((2,)), dma((4,)),
                dma((4, 2)), dma((4, 2)), dma((4, 2)), dma((4, 2)), dma((4, 2)),
                dma((8, 2)), dma((8, 2)), dma((8, 2)), dma((8, 2)), dma((8,)), dma((8,)),
            ],
            compiler_params=pltpu.CompilerParams(
                collective_id=0, has_side_effects=True, vmem_limit_bytes=60 * 1024 * 1024
            ),
        )(a, g)

    spec = P(("rep", "dp"), None, None, None)
    return jax.shard_map(
        body, mesh=mesh, in_specs=(spec, spec), out_specs=P("rep", None, None), check_vma=False
    )
```

time: 1450 us -> 553 us (0.38)
  blocking collectives: 1200 us -> 0 us
  Pallas kernels: 0 us -> 518 us
  matrix products: 249 us -> 0 us
  local copies, waits for them, and re-layouts: 0 us -> 34.6 us
    dot_general x1 -> x0, blocking collectives: 1200 us -> none  [step(): jnp.einsum('rsntd,rsntf->rndf', a, g, preferred_element_type=jnp.float32)]
    pallas_call x0 -> x1, Pallas kernels: none -> 518 us  [body(): pl.pallas_call(_kernel, out_shape=jax.ShapeDtypeStruct((mats, rows, cols)...]
    dot_general x1 -> x0, matrix products: 249 us -> none  [step(): jnp.einsum('rsntd,rsntf->rndf', a, g, preferred_element_type=jnp.float32)]
    unnamed x0 -> x1, local copies, waits for them, and re-layouts: none -> 34.6 us
where the time goes in v1:
time: 553 us
  Pallas kernels  518 us (94%)
  local copies, waits for them, and re-layouts  34.6 us (6%)
    pallas_call x1, Pallas kernels, body(): pl.pallas_call(_kernel, out_shape=jax.ShapeDtypeStruct((mats, rows, cols)...  518 us
    unnamed x1, local copies, waits for them, and re-layouts  34.6 us

profile of v1, /device:TPU:0, one launch (start us, length us, event | category | flops | bytes accessed | tf_op | source)
XLA Modules:
  0.0 552.6 jit_solution(10707941383906276667)
XLA Ops:
  0.0 518.0 %shard_map.28 = bf16[4,1536,4224]{2,1,0:T(8,128)(2,1)} custom-call(bf16[1,4,4096,1536]{3,2,1,0:T(8,128)(2,1)} %a.1, bf16[1,4,4096,4224]{3,2,1,0:T(8,128)(2,1)} %g.1), custom_call_target="tpu_custom_call" | custom-call | tf_op jit(solution)/shard_map/pallas_call | solution.py:247
  518.0 34.6 %copy.4 = bf16[4,1536,4224]{2,1,0:T(8,128)(2,1)} copy(bf16[4,1536,4224]{2,1,0:T(8,128)(2,1)} %shard_map.28) | data formatting | bytes 103809024

commit v2 on v1

--- a/solution.py
+++ b/solution.py
@@ -9,12 +9,13 @@
 W = 256
 G_SLOTS = 3
 F32, BF16 = jnp.float32, jnp.bfloat16
-LAG2, LAG3, LAG4, LAG5, LAG6 = 1, 2, 3, 5, 7
+LAG1, LAG2, LAG3, LAG4, LAG5, LAG6 = 0, 1, 2, 3, 5, 7
+PAIRS, KEEPS, RING, SEMS = 2, 2, 4, 8
 
 
 def _kernel(
     a, g, out,
-    a_buf, g_buf, pair_send, own, pair_recv,
+    a_buf, g_buf, pair_send, product, pair_recv,
     send1, keep1, recv1, send2, keep2, recv2, fin,
     a_sem, g_sem, pair_ss, pair_rs, ss1, rs1, ss2, rs2, loc, gs1, gr1, gs2, gr2, fs, fr,
 ):
@@ -70,20 +71,20 @@
         )
 
     def pair(k, w):
-        s, r = lax.rem(k, 2), lax.rem(k, 4)
+        s, r = lax.rem(k, PAIRS), lax.rem(k, RING)
         return remote(
             pair_send.at[s, :, pl.ds(0, w)], pair_recv.at[r, :, pl.ds(0, w)], pair_ss.at[s], pair_rs.at[r], pn
         )
 
     def scatter1(k, w):
-        s = lax.rem(k, 4)
+        s = lax.rem(k, RING)
         return [
             remote(send1.at[s, i, :, pl.ds(0, w)], recv1.at[s, i, :, pl.ds(0, w)], ss1.at[s, i], rs1.at[s, i], d)
             for i, d in enumerate((xn, yn))
         ]
 
     def scatter2(k, w):
-        s = lax.rem(k, 4)
+        s = lax.rem(k, RING)
         return [
             remote(send2.at[s, i, :, pl.ds(0, w)], recv2.at[s, i, :, pl.ds(0, w)], ss2.at[s, i], rs2.at[s, i], d)
             for i, d in enumerate((yn, xn))
@@ -93,28 +94,28 @@
         return (base + p_mine + eighth * y, base + q_mine + eighth * x)
 
     def keep_local(k, w):
-        s = lax.rem(k, 4)
+        s = lax.rem(k, RING)
         return [
             pltpu.make_async_copy(fin.at[s, i, :, pl.ds(0, w)], where(k, w, r, eighth), loc.at[s, i])
             for i, r in enumerate(final_rows())
         ]
 
     def gather1(k, w):
-        s, t = lax.rem(k, 4), lax.rem(k, 8)
+        s, t = lax.rem(k, RING), lax.rem(k, SEMS)
         return [
             remote(fin.at[s, i, :, pl.ds(0, w)], where(k, w, r, eighth), gs1.at[t, i], gr1.at[t, i], d)
             for i, (r, d) in enumerate(zip(final_rows(), (yn, xn)))
         ]
 
     def gather2(k, w):
-        t = lax.rem(k, 8)
+        t = lax.rem(k, SEMS)
         return [
             remote(where(k, w, r, quarter), where(k, w, r, quarter), gs2.at[t, i], gr2.at[t, i], d)
             for i, (r, d) in enumerate(((base + p_mine, xn), (base + q_mine, yn)))
         ]
 
     def exchange(k, w):
-        t = lax.rem(k, 8)
+        t = lax.rem(k, SEMS)
         return remote(where(k, w, base, half), where(k, w, base, half), fs.at[t], fr.at[t], pn)
 
     def matmul(k, h):
@@ -149,19 +150,26 @@
             load_a(n + 1, 1 - c).start()
             load_a(n + 1, c).start()
 
-        pl.when(j == 0)(lambda: load_a(n, 1 - c).wait())
         by_width(k, lambda w: load_g(k, w).wait())
-        pair_send[lax.rem(k, 2)] = matmul(k, 1 - c).astype(BF16)
-        by_width(k, lambda w: pair(k, w).start())
-        pl.when(j == 0)(lambda: load_a(n, c).wait())
-        own[...] = matmul(k, c)
-
+
+        @pl.loop(0, 2)
+        def _(t):
+            h = lax.rem(1 - c + t, 2)
+            pl.when(j == 0)(lambda: load_a(n, h).wait())
+            product[t] = matmul(k, h)
+
+            @pl.when(t == 0)
+            def _():
+                pair_send[lax.rem(k, PAIRS)] = product[0].astype(BF16)
+                by_width(k, lambda w: pair(k, w).start())
+
+    def first(k):
         by_width(k, lambda w: pair(k, w).wait_recv())
-        r, s, kept = lax.rem(k, 4), lax.rem(k, 4), lax.rem(k, 2)
-
-        def total(first):
-            span = pl.ds(pl.multiple_of(first, quarter), quarter)
-            return own[span, :] + pair_recv[r, span, :].astype(F32)
+        r, s, kept = lax.rem(k, RING), lax.rem(k, RING), lax.rem(k, KEEPS)
+
+        def total(at):
+            span = pl.ds(pl.multiple_of(at, quarter), quarter)
+            return product[1, span, :] + pair_recv[r, span, :].astype(F32)
 
         send1[s, 0] = total(p_other).astype(BF16)
         send1[s, 1] = total(q_other).astype(BF16)
@@ -176,10 +184,10 @@
                 copy.wait_recv()
 
         by_width(k, wait)
-        s, kept = lax.rem(k, 4), lax.rem(k, 2)
+        s, kept = lax.rem(k, RING), lax.rem(k, KEEPS)
         for i, bit in enumerate((y, x)):
-            def total(first):
-                span = pl.ds(pl.multiple_of(first, eighth), eighth)
+            def total(at):
+                span = pl.ds(pl.multiple_of(at, eighth), eighth)
                 return keep1[kept, i, span, :] + recv1[s, i, span, :].astype(F32)
 
             send2[s, i] = total(eighth * (1 - bit)).astype(BF16)
@@ -194,7 +202,7 @@
                 copy.wait_recv()
 
         by_width(k, wait)
-        s, kept = lax.rem(k, 4), lax.rem(k, 2)
+        s, kept = lax.rem(k, RING), lax.rem(k, KEEPS)
         for i in range(2):
             fin[s, i] = (keep2[kept, i] + recv2[s, i].astype(F32)).astype(BF16)
         by_width(k, lambda w: start(gather1(k, w) + keep_local(k, w)))
@@ -232,7 +240,7 @@
     @pl.loop(0, chunks + LAG6)
     def _(i):
         pl.when(i < chunks)(lambda: compute(i))
-        for lag, stage in ((LAG2, second), (LAG3, third), (LAG4, fourth), (LAG5, fifth), (LAG6, sixth)):
+        for lag, stage in ((LAG1, first), (LAG2, second), (LAG3, third), (LAG4, fourth), (LAG5, fifth), (LAG6, sixth)):
             pl.when((i >= lag) & (i < chunks + lag))(lambda lag=lag, stage=stage: stage(i - lag))
 
 
@@ -252,19 +260,19 @@
             scratch_shapes=[
                 pltpu.VMEM((2, tokens, rows), BF16),
                 pltpu.VMEM((G_SLOTS, tokens, W), BF16),
-                pltpu.VMEM((2, half, W), BF16),
-                pltpu.VMEM((half, W), F32),
-                pltpu.VMEM((4, half, W), BF16),
-                pltpu.VMEM((4, 2, quarter, W), BF16),
-                pltpu.VMEM((2, 2, quarter, W), F32),
-                pltpu.VMEM((4, 2, quarter, W), BF16),
-                pltpu.VMEM((4, 2, eighth, W), BF16),
-                pltpu.VMEM((2, 2, eighth, W), F32),
-                pltpu.VMEM((4, 2, eighth, W), BF16),
-                pltpu.VMEM((4, 2, eighth, W), BF16),
-                dma((2, 2)), dma((G_SLOTS,)), dma((2,)), dma((4,)),
-                dma((4, 2)), dma((4, 2)), dma((4, 2)), dma((4, 2)), dma((4, 2)),
-                dma((8, 2)), dma((8, 2)), dma((8, 2)), dma((8, 2)), dma((8,)), dma((8,)),
+                pltpu.VMEM((PAIRS, half, W), BF16),
+                pltpu.VMEM((2, half, W), F32),
+                pltpu.VMEM((RING, half, W), BF16),
+                pltpu.VMEM((RING, 2, quarter, W), BF16),
+                pltpu.VMEM((KEEPS, 2, quarter, W), F32),
+                pltpu.VMEM((RING, 2, quarter, W), BF16),
+                pltpu.VMEM((RING, 2, eighth, W), BF16),
+                pltpu.VMEM((KEEPS, 2, eighth, W), F32),
+                pltpu.VMEM((RING, 2, eighth, W), BF16),
+                pltpu.VMEM((RING, 2, eighth, W), BF16),
+                dma((2, 2)), dma((G_SLOTS,)), dma((PAIRS,)), dma((RING,)),
+                dma((RING, 2)), dma((RING, 2)), dma((RING, 2)), dma((RING, 2)), dma((RING, 2)),
+                dma((SEMS, 2)), dma((SEMS, 2)), dma((SEMS, 2)), dma((SEMS, 2)), dma((SEMS,)), dma((SEMS,)),
             ],
             compiler_params=pltpu.CompilerParams(
                 collective_id=0, has_side_effects=True, vmem_limit_bytes=60 * 1024 * 1024

time: 553 us -> 469 us (0.85)
  Pallas kernels: 518 us -> 435 us
    pallas_call x1, Pallas kernels: 518 us -> 435 us  [body(): pl.pallas_call(_kernel, out_shape=jax.ShapeDtypeStruct((mats, rows, cols)...]
where the time goes in v2:
time: 469 us
  Pallas kernels  435 us (93%)
  local copies, waits for them, and re-layouts  34.6 us (7%)
    pallas_call x1, Pallas kernels, body(): pl.pallas_call(_kernel, out_shape=jax.ShapeDtypeStruct((mats, rows, cols)...  435 us
    unnamed x1, local copies, waits for them, and re-layouts  34.6 us

profile of v2, /device:TPU:0, one launch (start us, length us, event | category | flops | bytes accessed | tf_op | source)
XLA Modules:
  0.0 469.4 jit_solution(10880910194324561772)
XLA Ops:
  0.0 434.7 %shard_map.28 = bf16[4,1536,4224]{2,1,0:T(8,128)(2,1)} custom-call(bf16[1,4,4096,1536]{3,2,1,0:T(8,128)(2,1)} %a.1, bf16[1,4,4096,4224]{3,2,1,0:T(8,128)(2,1)} %g.1), custom_call_target="tpu_custom_call" | custom-call | tf_op jit(solution)/shard_map/pallas_call | solution.py:255
  434.8 34.6 %copy.4 = bf16[4,1536,4224]{2,1,0:T(8,128)(2,1)} copy(bf16[4,1536,4224]{2,1,0:T(8,128)(2,1)} %shard_map.28) | data formatting | bytes 103809024

commit v3 on v2

--- a/solution.py
+++ b/solution.py
@@ -1,3 +1,5 @@
+import functools
+
 import jax
 import jax.numpy as jnp
 from jax import lax
@@ -5,26 +7,32 @@
 from jax.experimental.pallas import tpu as pltpu
 from jax.sharding import PartitionSpec as P
 
+
 MESH = pl.DeviceIdType.MESH
 W = 256
 G_SLOTS = 3
 F32, BF16 = jnp.float32, jnp.bfloat16
-LAG1, LAG2, LAG3, LAG4, LAG5, LAG6 = 0, 1, 2, 3, 5, 7
+VMEM = 67_043_328
+BLOCK, BLOCKS = 192, 16
+SEGMENT = 3072
+FLOPS_PER_US = 500_000_000
+LAG1, LAG2, LAG3, LAG4, LAG5, LAG6, LAG7 = 0, 1, 2, 3, 3, 5, 7
+PACE = 4
 PAIRS, KEEPS, RING, SEMS = 2, 2, 4, 8
 
 
 def _kernel(
-    a, g, out,
+    a, g, out, last_x0, last_y0, last_x1, last_y1,
     a_buf, g_buf, pair_send, product, pair_recv,
     send1, keep1, recv1, send2, keep2, recv2, fin,
     a_sem, g_sem, pair_ss, pair_rs, ss1, rs1, ss2, rs2, loc, gs1, gr1, gs2, gr2, fs, fr,
 ):
-    mats, rows, cols = out.shape
+    mats, (_, rows, cols) = a.shape[1], out.shape
     half, quarter = rows // 2, rows // 8
     eighth = quarter // 2
     per = pl.cdiv(cols, W)
     last_w = cols - (per - 1) * W
-    chunks = mats * per
+    chunks, done = mats * per, (mats - 1) * per
 
     me = lax.axis_index("dp")
     c, y, x = lax.rem(me, 2), lax.rem(me // 2, 2), me // 4
@@ -58,6 +66,11 @@
             src_ref=src, dst_ref=dst, send_sem=ss, recv_sem=rs, device_id=to, device_id_type=MESH
         )
 
+    def by_case(k, fn):
+        pl.when(k < done)(lambda: by_width(k, lambda w: fn(w, None)))
+        pl.when((k >= done) & (k < done + SEGMENT // W))(lambda: fn(W, 0))
+        pl.when(k >= done + SEGMENT // W)(lambda: by_width(k, lambda w: fn(w, 1)))
+
     def load_a(n, h):
         lanes = pl.ds(pl.multiple_of(h * half, half), half)
         slot = lax.rem(n, 2)
@@ -90,21 +103,28 @@
             for i, d in enumerate((yn, xn))
         ]
 
-    def final_rows():
-        return (base + p_mine + eighth * y, base + q_mine + eighth * x)
-
-    def keep_local(k, w):
+    def final_places(k, w, tail):
+        if tail is not None:
+            col = pl.multiple_of(lax.rem(k, per) * W - SEGMENT * tail, W)
+            refs = ((last_x0, last_y0), (last_x1, last_y1))[tail]
+            return [
+                ref.at[pl.ds(pl.multiple_of(eighth * bit, eighth), eighth), pl.ds(col, w)]
+                for ref, bit in zip(refs, (y, x))
+            ]
+        return [where(k, w, r, eighth) for r in (base + p_mine + eighth * y, base + q_mine + eighth * x)]
+
+    def keep_local(k, w, tail):
         s = lax.rem(k, RING)
         return [
-            pltpu.make_async_copy(fin.at[s, i, :, pl.ds(0, w)], where(k, w, r, eighth), loc.at[s, i])
-            for i, r in enumerate(final_rows())
-        ]
-
-    def gather1(k, w):
+            pltpu.make_async_copy(fin.at[s, i, :, pl.ds(0, w)], place, loc.at[s, i])
+            for i, place in enumerate(final_places(k, w, tail))
+        ]
+
+    def gather1(k, w, tail):
         s, t = lax.rem(k, RING), lax.rem(k, SEMS)
         return [
-            remote(fin.at[s, i, :, pl.ds(0, w)], where(k, w, r, eighth), gs1.at[t, i], gr1.at[t, i], d)
-            for i, (r, d) in enumerate(zip(final_rows(), (yn, xn)))
+            remote(fin.at[s, i, :, pl.ds(0, w)], place, gs1.at[t, i], gr1.at[t, i], d)
+            for i, (place, d) in enumerate(zip(final_places(k, w, tail), (yn, xn)))
         ]
 
     def gather2(k, w):
@@ -205,31 +225,29 @@
         s, kept = lax.rem(k, RING), lax.rem(k, KEEPS)
         for i in range(2):
             fin[s, i] = (keep2[kept, i] + recv2[s, i].astype(F32)).astype(BF16)
-        by_width(k, lambda w: start(gather1(k, w) + keep_local(k, w)))
+        by_case(k, lambda w, tail: start(gather1(k, w, tail) + keep_local(k, w, tail)))
 
     def fourth(k):
-        def go(w):
+        def go(w, tail):
             for copy in scatter2(k, w):
                 copy.wait_send()
-            for copy in keep_local(k, w):
+            for copy in keep_local(k, w, tail) + gather1(k, w, tail):
                 copy.wait()
-            for copy in gather1(k, w):
-                copy.wait_recv()
-            start(gather2(k, w))
-
-        by_width(k, go)
+
+        by_case(k, go)
 
     def fifth(k):
+        by_width(k, lambda w: start(gather2(k, w)))
+
+    def sixth(k):
         def go(w):
-            for copy in gather1(k, w):
-                copy.wait_send()
             for copy in gather2(k, w):
                 copy.wait_recv()
             exchange(k, w).start()
 
         by_width(k, go)
 
-    def sixth(k):
+    def seventh(k):
         def go(w):
             for copy in gather2(k, w):
                 copy.wait_send()
@@ -237,26 +255,113 @@
 
         by_width(k, go)
 
-    @pl.loop(0, chunks + LAG6)
+    paced = done // (PACE - 1) * PACE + done % (PACE - 1)
+
+    @pl.loop(0, max(chunks + LAG4, paced + LAG7))
     def _(i):
         pl.when(i < chunks)(lambda: compute(i))
-        for lag, stage in ((LAG1, first), (LAG2, second), (LAG3, third), (LAG4, fourth), (LAG5, fifth), (LAG6, sixth)):
+        for lag, stage in ((LAG1, first), (LAG2, second), (LAG3, third), (LAG4, fourth)):
             pl.when((i >= lag) & (i < chunks + lag))(lambda lag=lag, stage=stage: stage(i - lag))
+        for lag, stage in ((LAG5, fifth), (LAG6, sixth), (LAG7, seventh)):
+            @pl.when((i >= lag) & (i < paced + lag) & (lax.rem(i + PACE - lag, PACE) < PACE - 1))
+            def _(lag=lag, stage=stage):
+                u = i - lag
+                stage(u // PACE * (PACE - 1) + lax.rem(u, PACE))
+
+
+def _move(loads, stores, slots):
+    for i in range(len(loads) + slots):
+        if 0 <= i - slots:
+            stores[i - slots].wait()
+        if i < len(loads):
+            loads[i].start()
+        j = i - slots // 2
+        if 0 <= j < len(loads):
+            loads[j].wait()
+            stores[j].start()
+
+
+def _rows(kind, out, size):
+    by, others, theirs, col = kind
+    quarter, width = size
+    me = lax.axis_index("dp")
+    c, bit = lax.rem(me, 2), lax.rem(me // 2, 2) if by else me // 4
+    bit = 1 - bit if others else bit
+    row = 4 * quarter * (1 - c if theirs else c) + 2 * quarter * by + quarter * bit
+    return out.at[out.shape[0] - 1, pl.ds(pl.multiple_of(row, quarter), quarter), pl.ds(col, width)]
+
+
+def _copy(kinds, sums, *refs):
+    blocks, (out, buf, in_sem, out_sem) = refs[: len(kinds)], refs[len(kinds) :]
+    sources, targets, loads, stores = [], [], [], []
+    for n in range(sums.shape[0]):
+        for r in range(0, sums.shape[1], BLOCK):
+            sources.append(sums.at[n, pl.ds(r, BLOCK)])
+            targets.append(out.at[n, pl.ds(r, BLOCK)])
+    for kind, block in zip(kinds, blocks):
+        sources.append(block)
+        targets.append(_rows(kind, out, block.shape))
+    for i, (source, target) in enumerate(zip(sources, targets)):
+        slot = i % BLOCKS
+        part = buf.at[slot, :, pl.ds(0, source.shape[1])]
+        loads.append(pltpu.make_async_copy(source, part, in_sem.at[slot]))
+        stores.append(pltpu.make_async_copy(part, target, out_sem.at[slot]))
+    _move(loads, stores, BLOCKS)
+
+
+def _place(kinds, *refs):
+    count = len(kinds)
+    blocks, out, bufs, (in_sem, out_sem) = refs[:count], refs[count + 1], refs[count + 2 : -2], refs[-2:]
+    loads, stores = [], []
+    for i, (kind, block, buf) in enumerate(zip(kinds, blocks, bufs)):
+        loads.append(pltpu.make_async_copy(block, buf, in_sem.at[i]))
+        stores.append(pltpu.make_async_copy(buf, _rows(kind, out, block.shape), out_sem.at[i]))
+    for load in loads:
+        load.start()
+    for load, store in zip(loads, stores):
+        load.wait()
+        store.start()
+    for store in stores:
+        store.wait()
 
 
 def solution(mesh):
+    any_space = pl.BlockSpec(memory_space=pl.ANY)
+    dma = pltpu.SemaphoreType.DMA
+    devices = mesh.shape["dp"]
+
+    def swap(t, bit):
+        return lax.ppermute(t, "dp", [(i, i ^ bit) for i in range(devices)])
+
+    def place(out, named):
+        kinds, blocks = zip(*named)
+        return pl.pallas_call(
+            functools.partial(_place, kinds),
+            out_shape=jax.ShapeDtypeStruct(out.shape, out.dtype),
+            in_specs=[any_space] * (len(blocks) + 1),
+            out_specs=any_space,
+            scratch_shapes=[pltpu.VMEM(t.shape, t.dtype) for t in blocks] + [dma((len(blocks),))] * 2,
+            input_output_aliases={len(blocks): 0},
+            compiler_params=pltpu.CompilerParams(vmem_limit_bytes=VMEM),
+            cost_estimate=pl.CostEstimate(
+                flops=FLOPS_PER_US * 3, bytes_accessed=4 * sum(t.size for t in blocks), transcendentals=0
+            ),
+        )(*blocks, out)
+
     def body(a, g):
         mats, tokens, rows = a.shape[1:]
         cols = g.shape[-1]
         half, quarter = rows // 2, rows // 8
         eighth = quarter // 2
-        dma = pltpu.SemaphoreType.DMA
-        any_space = pl.BlockSpec(memory_space=pl.ANY)
-        return pl.pallas_call(
+        lasts = [
+            jax.ShapeDtypeStruct((quarter, width), BF16)
+            for width in (SEGMENT, SEGMENT, cols - SEGMENT, cols - SEGMENT)
+        ]
+        sums, *lasts = pl.pallas_call(
             _kernel,
-            out_shape=jax.ShapeDtypeStruct((mats, rows, cols), BF16),
+            out_shape=[jax.ShapeDtypeStruct((mats - 1, rows, cols), BF16)] + lasts,
             in_specs=[any_space, any_space],
-            out_specs=any_space,
+            out_specs=[any_space] * 5,
             scratch_shapes=[
                 pltpu.VMEM((2, tokens, rows), BF16),
                 pltpu.VMEM((G_SLOTS, tokens, W), BF16),
@@ -279,6 +384,33 @@
             ),
         )(a, g)
 
+        def kinds(part, others, theirs):
+            return [(by, others, theirs, SEGMENT * part) for by in range(2)]
+
+        mine = (lasts[:2], lasts[2:])
+        others = []
+        for part in range(2):
+            others.append([swap(t, bit) for t, bit in zip(mine[part], (4, 2))])
+        theirs = [[swap(t, 1) for t in mine[part]] for part in range(2)]
+        here = [n for p in range(2) for n in kinds(p, 0, 0)]
+        out = pl.pallas_call(
+            functools.partial(_copy, here),
+            out_shape=jax.ShapeDtypeStruct((mats, rows, cols), BF16),
+            in_specs=[any_space] * (1 + len(here)),
+            out_specs=any_space,
+            scratch_shapes=[pltpu.VMEM((BLOCKS, BLOCK, cols), BF16), dma((BLOCKS,)), dma((BLOCKS,))],
+            compiler_params=pltpu.CompilerParams(vmem_limit_bytes=VMEM),
+            cost_estimate=pl.CostEstimate(
+                flops=FLOPS_PER_US * 28, bytes_accessed=4 * (mats - 1) * rows * cols, transcendentals=0
+            ),
+        )(sums, *mine[0], *mine[1])
+        theirs0 = [swap(t, 1) for t in others[0]]
+        named = [n for p in range(2) for n in zip(kinds(p, 0, 1), theirs[p])]
+        out = place(out, named + list(zip(kinds(0, 1, 0), others[0])))
+        theirs1 = [swap(t, 1) for t in others[1]]
+        out = place(out, list(zip(kinds(0, 1, 1), theirs0)) + list(zip(kinds(1, 1, 0), others[1])))
+        return place(out, list(zip(kinds(1, 1, 1), theirs1)))
+
     spec = P(("rep", "dp"), None, None, None)
     return jax.shard_map(
         body, mesh=mesh, in_specs=(spec, spec), out_specs=P("rep", None, None), check_vma=False

time: 469 us -> 482 us (1.028)
  local copies, waits for them, and re-layouts: 34.6 us -> 0 us
  waiting for transfers between devices: 0 us -> 34.3 us
  Pallas kernels: 435 us -> 441 us
  starting transfers between devices: 0 us -> 5.61 us
    unnamed x1 -> x0, local copies, waits for them, and re-layouts: 34.6 us -> none
    ppermute x0 -> x12, waiting for transfers between devices: none -> 34.3 us  [swap(): return lax.ppermute(t, 'dp', [(i, i ^ bit) for i in range(devices)])]
    pallas_call x1 -> x5, Pallas kernels: 435 us -> 441 us  [the longest x1 404 us: body(): pl.pallas_call(_kernel, out_shape=[jax.ShapeDtypeStruct((mats - 1, rows,...]
    ppermute x0 -> x12, starting transfers between devices: none -> 5.61 us  [swap(): return lax.ppermute(t, 'dp', [(i, i ^ bit) for i in range(devices)])]
  transfers between devices with their start and end apart: 0 -> 12, of which waited for: 0 -> 3; matrix products, arithmetic and copies ran while one was open for 0% -> 0% of each run, Pallas kernels for 0% -> 7%
where the time goes in v3:
time: 482 us; the launch traced here: 481 us
  Pallas kernels  441 us (91%)
  waiting for transfers between devices  34.3 us (7%)
  starting transfers between devices  5.61 us (1%)
    pallas_call x1, Pallas kernels, body(): pl.pallas_call(_kernel, out_shape=[jax.ShapeDtypeStruct((mats - 1, rows,...  404 us
    ppermute x12, waiting for transfers between devices, swap(): return lax.ppermute(t, 'dp', [(i, i ^ bit) for i in range(devices)])  34.3 us
    pallas_call x1, Pallas kernels, body(): pl.pallas_call(functools.partial(_copy, here), out_shape=jax.ShapeDtypeSt...  27.8 us
    pallas_call x3, Pallas kernels, place(): pl.pallas_call(functools.partial(_place, kinds), out_shape=jax.ShapeDtype...  9.69 us
  transfers between devices with their start and end apart: 12, of which 3 were waited for; matrix products, arithmetic and copies ran while one was open for 0% of the time, Pallas kernels for 7%

profile of v3, /device:TPU:0, one launch (start us, length us, event | category | flops | bytes accessed | tf_op | source)
XLA Modules:
  0.0 481.4 jit_solution(10198913292661914681)
XLA Ops:
  0.0 403.9 %shard_map.28 = (bf16[3,1536,4224]{2,1,0:T(8,128)(2,1)}, bf16[192,3072]{1,0:T(8,128)(2,1)}, bf16[192,3072]{1,0:T(8,128)(2,1)}, bf16[192,1152]{1,0:T(8,128)(2,1)}, bf16[192,1152]{1,0:T(8,128)(2,1)}) custom-call(bf16[1,4,4096,1536]{3,2,1,0:T(8,128)(2,1)} %a.1, bf16[1,4,4096,4224]{3,2,1,0:T(8,128)(2,1)} %g.1), custom_call_target="tpu_custom_call" | custom-call | tf_op jit(solution)/shard_map/pallas_call | solution.py:360
  403.9 1.1 collective-permute-start.4
  405.0 1.0 collective-permute-start.6
  406.0 0.0 collective-permute-start.8
  406.0 0.5 collective-permute-start.10
  406.5 0.0 collective-permute-start.11
  406.5 3.3 collective-permute-done.10.refs_2_
  409.8 1.1 collective-permute-start
  410.8 0.0 collective-permute-done.11.refs_3_
  410.9 1.0 collective-permute-start.2
  411.8 30.2 %collective-permute-done.refs_2_ = bf16[192,1152]{1,0:T(8,128)(2,1)} collective-permute-done((bf16[192,1152]{1,0:T(8,128)(2,1)}, bf16[192,1152]{1,0:T(8,128)(2,1)}, u32[]{:S(2)}, u32[]{:S(2)}) %collective-permute-start) | collective-permute-done | bytes 442400 | tf_op jit(solution)/shard_map/ppermute | solution.py:334
  442.0 0.0 collective-permute-start.9
  442.0 0.8 collective-permute-done.2.refs_3_
  442.8 0.0 collective-permute-start.1
  442.8 0.0 collective-permute-done.4.refs_4_
  442.8 0.5 collective-permute-start.3
  443.3 0.0 collective-permute-done.6.refs_5_
  443.3 0.0 collective-permute-start.5
  443.3 0.0 collective-permute-done.8.refs_0_
  443.3 0.5 collective-permute-start.7
  443.8 27.8 %shard_map.29.refs_6_ = bf16[4,1536,4224]{2,1,0:T(8,128)(2,1)} custom-call(bf16[3,1536,4224]{2,1,0:T(8,128)(2,1)} %get-tuple-element.14.sums, bf16[192,3072]{1,0:T(8,128)(2,1)} %get-tuple-element.12.refs_0_, bf16[192,3072]{1,0:T(8,128)(2,1)} %get-tuple-element.13.refs_1_, bf16[192,1152]{1,0:T(8,128)(2,1)} %get-tuple-element.10.refs_2_, ...), custom_call_target="tpu_custom_call" | custom-call | flops 14000000000 | bytes 77856768 | tf_op jit(solution)/shard_map/pallas_call | solution.py:396
  471.6 0.0 collective-permute-done.9.refs_1_
  471.7 4.7 shard_map.30.refs_4_
  476.4 0.0 collective-permute-done.5.refs_0_
  476.4 0.0 collective-permute-done.7.refs_1_
  476.4 3.0 shard_map.31.refs_2_
  479.4 0.0 collective-permute-done.1.refs_0_
  479.4 0.0 collective-permute-done.3.refs_1_
  479.4 2.0 shard_map.32
Async XLA Ops:
  403.9 38.8 %collective-permute-start.4 = (bf16[192,3072]{1,0:T(8,128)(2,1)}, bf16[192,3072]{1,0:T(8,128)(2,1)}, u32[]{:S(2)}, u32[]{:S(2)}) collective-permute-start(bf16[192,3072]{1,0:T(8,128)(2,1)} %get-tuple-element.12.refs_0_), channel_id=1, source_target_pairs={{0,4},{1,5},{2,6},{3,7},{4,0},{5,1},{6,2},{7,3}} | collective-permute-start | bytes 3538952 | tf_op jit(solution)/shard_map/ppermute | solution.py:334
  405.0 38.3 %collective-permute-start.6 = (bf16[192,3072]{1,0:T(8,128)(2,1)}, bf16[192,3072]{1,0:T(8,128)(2,1)}, u32[]{:S(2)}, u32[]{:S(2)}) collective-permute-start(bf16[192,3072]{1,0:T(8,128)(2,1)} %get-tuple-element.13.refs_1_), channel_id=1, source_target_pairs={{0,2},{1,3},{2,0},{3,1},{4,6},{5,7},{6,4},{7,5}} | collective-permute-start | bytes 3538952 | tf_op jit(solution)/shard_map/ppermute | solution.py:334
  406.0 37.3 %collective-permute-start.8 = (bf16[192,3072]{1,0:T(8,128)(2,1)}, bf16[192,3072]{1,0:T(8,128)(2,1)}, u32[]{:S(2)}, u32[]{:S(2)}) collective-permute-start(bf16[192,3072]{1,0:T(8,128)(2,1)} %get-tuple-element.12.refs_0_), channel_id=1, source_target_pairs={{0,1},{1,0},{2,3},{3,2},{4,5},{5,4},{6,7},{7,6}} | collective-permute-start | bytes 3538952 | tf_op jit(solution)/shard_map/ppermute | solution.py:334
  406.0 3.8 collective-permute-start.10
  406.5 4.4 collective-permute-start.11
  409.8 32.2 %collective-permute-start = (bf16[192,1152]{1,0:T(8,128)(2,1)}, bf16[192,1152]{1,0:T(8,128)(2,1)}, u32[]{:S(2)}, u32[]{:S(2)}) collective-permute-start(bf16[192,1152]{1,0:T(8,128)(2,1)} %get-tuple-element.10.refs_2_), channel_id=1, source_target_pairs={{0,4},{1,5},{2,6},{3,7},{4,0},{5,1},{6,2},{7,3}} | collective-permute-start | bytes 1327112 | tf_op jit(solution)/shard_map/ppermute | solution.py:334
  410.9 31.9 %collective-permute-start.2 = (bf16[192,1152]{1,0:T(8,128)(2,1)}, bf16[192,1152]{1,0:T(8,128)(2,1)}, u32[]{:S(2)}, u32[]{:S(2)}) collective-permute-start(bf16[192,1152]{1,0:T(8,128)(2,1)} %get-tuple-element.11.refs_3_), channel_id=1, source_target_pairs={{0,2},{1,3},{2,0},{3,1},{4,6},{5,7},{6,4},{7,5}} | collective-permute-start | bytes 1327112 | tf_op jit(solution)/shard_map/ppermute | solution.py:334
  442.0 29.7 %collective-permute-start.9 = (bf16[192,3072]{1,0:T(8,128)(2,1)}, bf16[192,3072]{1,0:T(8,128)(2,1)}, u32[]{:S(2)}, u32[]{:S(2)}) collective-permute-start(bf16[192,3072]{1,0:T(8,128)(2,1)} %get-tuple-element.13.refs_1_), channel_id=1, source_target_pairs={{0,1},{1,0},{2,3},{3,2},{4,5},{5,4},{6,7},{7,6}} | collective-permute-start | bytes 3538952 | tf_op jit(solution)/shard_map/ppermute | solution.py:334
  442.8 36.7 %collective-permute-start.1 = (bf16[192,1152]{1,0:T(8,128)(2,1)}, bf16[192,1152]{1,0:T(8,128)(2,1)}, u32[]{:S(2)}, u32[]{:S(2)}) collective-permute-start(bf16[192,1152]{1,0:T(8,128)(2,1)} %collective-permute-done.refs_2_), channel_id=1, source_target_pairs={{0,1},{1,0},{2,3},{3,2},{4,5},{5,4},{6,7},{7,6}} | collective-permute-start | bytes 1327112 | tf_op jit(solution)/shard_map/ppermute | solution.py:334
  442.8 36.7 %collective-permute-start.3 = (bf16[192,1152]{1,0:T(8,128)(2,1)}, bf16[192,1152]{1,0:T(8,128)(2,1)}, u32[]{:S(2)}, u32[]{:S(2)}) collective-permute-start(bf16[192,1152]{1,0:T(8,128)(2,1)} %collective-permute-done.2.refs_3_), channel_id=1, source_target_pairs={{0,1},{1,0},{2,3},{3,2},{4,5},{5,4},{6,7},{7,6}} | collective-permute-start | bytes 1327112 | tf_op jit(solution)/shard_map/ppermute | solution.py:334
  443.3 33.1 %collective-permute-start.5 = (bf16[192,3072]{1,0:T(8,128)(2,1)}, bf16[192,3072]{1,0:T(8,128)(2,1)}, u32[]{:S(2)}, u32[]{:S(2)}) collective-permute-start(bf16[192,3072]{1,0:T(8,128)(2,1)} %collective-permute-done.4.refs_4_), channel_id=1, source_target_pairs={{0,1},{1,0},{2,3},{3,2},{4,5},{5,4},{6,7},{7,6}} | collective-permute-start | bytes 3538952 | tf_op jit(solution)/shard_map/ppermute | solution.py:334
  443.3 33.1 %collective-permute-start.7 = (bf16[192,3072]{1,0:T(8,128)(2,1)}, bf16[192,3072]{1,0:T(8,128)(2,1)}, u32[]{:S(2)}, u32[]{:S(2)}) collective-permute-start(bf16[192,3072]{1,0:T(8,128)(2,1)} %collective-permute-done.6.refs_5_), channel_id=1, source_target_pairs={{0,1},{1,0},{2,3},{3,2},{4,5},{5,4},{6,7},{7,6}} | collective-permute-start | bytes 3538952 | tf_op jit(solution)/shard_map/ppermute | solution.py:334
